TPU v7x, 32 devices: a whole 2x2x4 slice. The times are simulated.
32 devices in a mesh: section: 2 (over y), row: 4 (over z), col: 4 (over x, core).
Axes of the slice: x: 2, y: 2, z: 4, core: 2. Of those that a mesh axis runs over, the one named last changes fastest.
Arguments:
- tokens: bfloat16 [2, 256, 6144], P(None, 'col', 'row'), may hold values from -6 to 6
- ln_gain: float32 [2, 6144], P('section', 'row'), may hold values from 0.1 to 1.9
- w_query: bfloat16 [2, 6144, 6144], P('section', 'row', 'col'), as said below
- w_key: bfloat16 [2, 6144, 6144], P('section', 'row', 'col'), as said below
- w_value: bfloat16 [2, 6144, 6144], P('section', 'row', 'col'), may hold values from -0.078125 to 0.078125
- w_up: bfloat16 [2, 6144, 24576], P('section', 'row', 'col'), may hold values from -0.078125 to 0.078125
- w_out: bfloat16 [2, 6144, 6144], P('section', 'col', 'row'), may hold values from -0.078125 to 0.078125
- w_down: bfloat16 [2, 24576, 6144], P('section', 'col', 'row'), may hold values from -0.0390625 to 0.0390625
Outputs:
- section_out: bfloat16 [2, 2, 256, 6144], P('section', None, 'col', 'row')
Inputs may be any that keep to these rules, and one draw needn't show every extreme that they name: `w_query`: entries are normal with standard deviation 6144 ** -0.5, clipped at six deviations. `w_key`: entries are of the order of 6144 ** -0.5; in some heads the key columns may be up to twenty times larger and correlated with the query columns.
All inputs are finite; a program needn't handle non-finite values.
Results may differ from a plain program's by a relative error of at most 0.02.
Values may be sent and summed in bfloat16 or wider, within the bound.
A program may use at most 128 MiB of HBM per device.

v0:
```python
import jax
import jax.numpy as jnp
from jax import lax
from jax.sharding import PartitionSpec as P

D = 6144
HEADS = 48


EPS = 1e-06


def passed_along(value, axis, steps):
    count = lax.axis_size(axis)
    first, last = (max(0, -steps), min(count, count - steps))
    return lax.ppermute(value, axis, [(source, source + steps) for source in range(first, last)])


def layer(x, weights):
    gain, wq, wk, wv, wup, wout, wdown = weights
    xf = x.astype(jnp.float32)
    sums, squares = lax.psum((jnp.sum(xf, axis=-1), jnp.sum(xf * xf, axis=-1)), "row")
    mean = (sums / D)[..., None]
    var = jnp.maximum((squares / D)[..., None] - mean * mean, 0.0)
    normed = ((xf - mean) * lax.rsqrt(var + EPS) * gain).astype(jnp.bfloat16)
    gathered = lax.all_gather(normed, "col", axis=1, tiled=True)
    part_q = jnp.dot(gathered, wq, preferred_element_type=jnp.float32)
    part_k = jnp.dot(gathered, wk, preferred_element_type=jnp.float32)
    part_v = jnp.dot(gathered, wv, preferred_element_type=jnp.float32)
    part_m = jnp.dot(gathered, wup, preferred_element_type=jnp.float32)
    query, keyed, valued, pre = (
        lax.psum_scatter(
            part_q.astype(jnp.bfloat16), "row", scatter_dimension=1, tiled=True
        ).astype(jnp.float32),
        lax.psum_scatter(
            part_k.astype(jnp.bfloat16), "row", scatter_dimension=1, tiled=True
        ).astype(jnp.float32),
        lax.psum_scatter(
            part_v.astype(jnp.bfloat16), "row", scatter_dimension=1, tiled=True
        ).astype(jnp.float32),
        lax.psum_scatter(
            part_m.astype(jnp.bfloat16), "row", scatter_dimension=1, tiled=True
        ).astype(jnp.float32),
    )
    act = jax.nn.gelu(pre, approximate=False).astype(jnp.bfloat16)
    query = query.astype(jnp.bfloat16)
    keyed = keyed.astype(jnp.bfloat16)
    valued = valued.astype(jnp.bfloat16)
    all_keys, all_values = (
        lax.all_gather(keyed, "row", axis=1, tiled=True),
        lax.all_gather(valued, "row", axis=1, tiled=True),
    )
    head_dim = D // HEADS
    local_heads = query.shape[2] // head_dim
    images = query.shape[0]
    qh = query.reshape(images, query.shape[1], local_heads, head_dim)
    kh = all_keys.reshape(images, all_keys.shape[1], local_heads, head_dim)
    vh = all_values.reshape(images, all_values.shape[1], local_heads, head_dim)
    scores = jnp.einsum("bqhd,bkhd->bhqk", qh, kh, preferred_element_type=jnp.float32) / jnp.sqrt(
        jnp.float32(head_dim)
    )
    scores = scores - jnp.max(scores, axis=-1, keepdims=True)
    expo = jnp.exp(scores)
    probs = (expo / jnp.sum(expo, axis=-1, keepdims=True)).astype(jnp.bfloat16)
    attn = jnp.einsum("bhqk,bkhd->bqhd", probs, vh, preferred_element_type=jnp.float32)
    attn = attn.reshape(query.shape).astype(jnp.bfloat16)
    attn_full, act_full = (
        lax.all_gather(attn, "row", axis=1, tiled=True),
        lax.all_gather(act, "row", axis=1, tiled=True),
    )
    mixed = jnp.dot(attn_full, wout, preferred_element_type=jnp.float32) + jnp.dot(
        act_full, wdown, preferred_element_type=jnp.float32
    )
    summed = lax.psum_scatter(
        mixed.astype(jnp.bfloat16), "col", scatter_dimension=1, tiled=True
    ).astype(jnp.float32)
    return (xf + summed).astype(jnp.bfloat16)


def pass_on(output):
    return passed_along(output, "section", 1)


def local(tokens, ln_gain, w_query, w_key, w_value, w_up, w_out, w_down):
    weights = (ln_gain[0], w_query[0], w_key[0], w_value[0], w_up[0], w_out[0], w_down[0])
    section = lax.axis_index("section")
    sections = lax.axis_size("section")
    result = jnp.zeros_like(tokens)
    images = tokens.shape[0]
    ticks = images + sections - 1
    inbox = jnp.zeros_like(tokens[:1])
    positions = jnp.arange(images, dtype=jnp.int32)
    for tick in range(ticks):
        fresh = tokens[min(tick, images - 1) : min(tick, images - 1) + 1]
        current = jnp.where(section == 0, fresh, inbox)
        output = layer(current, weights)
        slot = tick - section
        result = jnp.where((positions == slot)[:, None, None], output, result)
        if tick + 1 < ticks:
            inbox = pass_on(output)
    return result[None]


def solution(mesh):
    return jax.shard_map(
        local,
        mesh=mesh,
        in_specs=(
            P(None, "col", "row"),
            P("section", "row"),
            P("section", "row", "col"),
            P("section", "row", "col"),
            P("section", "row", "col"),
            P("section", "row", "col"),
            P("section", "col", "row"),
            P("section", "col", "row"),
        ),
        out_specs=P("section", None, "col", "row"),
        check_vma=False,
    )
```

profile of v0, /device:TPU:0, one launch (start us, length us, event | category | flops | bytes accessed | tf_op | source)
XLA Modules:
  0.0 896.8 jit_solution(542227300804666971)
XLA Ops:
  7.6 13.5 %all-reduce.2 = (f32[1,64]{1,0:T(1,128)S(1)}, f32[1,64]{1,0:T(1,128)S(1)}) all-reduce(f32[1,64]{1,0:T(1,128)S(1)} %bitcast.283, f32[1,64]{1,0:T(1,128)S(1)} %bitcast.282), channel_id=1, replica_groups=mesh['section'=2,'row'=4,'col'=4] {'row'}, use_global_device_ids=true, to_apply=%region_3.4 | all-reduce | flops 128 | bytes 1024 | tf_op jit(solution)/shard_map/psum | solution.py:22
  31.5 12.8 %fusion.30 = bf16[1,256,6144]{2,1,0:T(8,128)(2,1)} fusion(bf16[1,1536,6144]{2,1,0:T(8,128)(2,1)} %param.13, bf16[1,256,1536]{2,1,0:T(8,128)(2,1)S(1)} %all_gather.45), kind=kOutput, calls=%fused_computation.20 | convolution fusion | flops 4833411072 | bytes 22806528 | tf_op jit(solution)/shard_map/dot_general | solution.py:30
  58.4 43.7 %reduce-scatter.22.cloned.1.call-done = bf16[1,64,6144]{2,1,0:T(8,128)(2,1)} async-done(((bf16[1,256,6144]{2,1,0:T(8,128)(2,1)}), bf16[1,64,6144]{2,1,0:T(8,128)(2,1)}) %reduce-scatter.22.cloned.1.call-update) | async-done | bytes 786448 | tf_op jit(solution)/shard_map/reduce_scatter | solution.py:41
  107.3 20.2 %reduce-scatter.20.cloned.1.call-done = bf16[1,64,1536]{2,1,0:T(8,128)(2,1)} async-done(((bf16[1,256,1536]{2,1,0:T(8,128)(2,1)}), bf16[1,64,1536]{2,1,0:T(8,128)(2,1)}) %reduce-scatter.20.cloned.1.call-update) | async-done | bytes 196624 | tf_op jit(solution)/shard_map/reduce_scatter | solution.py:35
  127.5 23.5 %all_gather.47 = bf16[1,256,1536]{2,1,0:T(8,128)(2,1)S(1)} all-gather(bf16[1,64,1536]{2,1,0:T(8,128)(2,1)} %reduce-scatter.20.cloned.1.call-done), channel_id=1, replica_groups=mesh['section'=2,'row'=4,'col'=4] {'row'}, dimensions={1}, use_global_device_ids=true | all-gather | bytes 983040 | tf_op jit(solution)/shard_map/all_gather | solution.py:50
  158.0 24.4 %all_gather.46 = bf16[1,256,1536]{2,1,0:T(8,128)(2,1)S(1)} all-gather(bf16[1,64,1536]{2,1,0:T(8,128)(2,1)} %reduce-scatter.16.cloned.1.call-done), channel_id=1, replica_groups=mesh['section'=2,'row'=4,'col'=4] {'row'}, dimensions={1}, use_global_device_ids=true | all-gather | bytes 983040 | tf_op jit(solution)/shard_map/all_gather | solution.py:51
  192.0 25.2 %all_gather.48 = bf16[1,256,1536]{2,1,0:T(8,128)(2,1)S(1)} all-gather(bf16[1,64,1536]{2,1,0:T(8,128)(2,1)S(1)} %bitcast.279), channel_id=1, replica_groups=mesh['section'=2,'row'=4,'col'=4] {'row'}, dimensions={1}, use_global_device_ids=true | all-gather | bytes 983040 | tf_op jit(solution)/shard_map/all_gather | solution.py:68
  217.2 42.8 %all-gather.4.cloned.1.call-done = bf16[1,256,6144]{2,1,0:T(8,128)(2,1)} async-done(((bf16[1,64,6144]{2,1,0:T(8,128)(2,1)}), bf16[1,256,6144]{2,1,0:T(8,128)(2,1)}) %all-gather.4.cloned.1.call-update) | async-done | bytes 3145744 | tf_op jit(solution)/shard_map/all_gather | solution.py:69
  274.6 22.5 %reduce-scatter.24.cloned.1.call-done = bf16[1,64,1536]{2,1,0:T(8,128)(2,1)} async-done(((bf16[1,256,1536]{2,1,0:T(8,128)(2,1)}), bf16[1,64,1536]{2,1,0:T(8,128)(2,1)}) %reduce-scatter.24.cloned.1.call-update) | async-done | bytes 196624 | tf_op jit(solution)/shard_map/reduce_scatter | solution.py:74
  325.2 12.8 %fusion.27 = bf16[1,256,6144]{2,1,0:T(8,128)(2,1)} fusion(bf16[1,1536,6144]{2,1,0:T(8,128)(2,1)} %param.13, bf16[1,256,1536]{2,1,0:T(8,128)(2,1)S(1)} %all_gather.50), kind=kOutput, calls=%fused_computation.19 | convolution fusion | flops 4833411072 | bytes 22806528 | tf_op jit(solution)/shard_map/dot_general | solution.py:30
  352.4 45.2 %reduce-scatter.32.cloned.1.call-done = bf16[1,64,6144]{2,1,0:T(8,128)(2,1)} async-done(((bf16[1,256,6144]{2,1,0:T(8,128)(2,1)}), bf16[1,64,6144]{2,1,0:T(8,128)(2,1)}) %reduce-scatter.32.cloned.1.call-update) | async-done | bytes 786448 | tf_op jit(solution)/shard_map/reduce_scatter | solution.py:41
  402.9 20.2 %reduce-scatter.30.cloned.1.call-done = bf16[1,64,1536]{2,1,0:T(8,128)(2,1)} async-done(((bf16[1,256,1536]{2,1,0:T(8,128)(2,1)}), bf16[1,64,1536]{2,1,0:T(8,128)(2,1)}) %reduce-scatter.30.cloned.1.call-update) | async-done | bytes 196624 | tf_op jit(solution)/shard_map/reduce_scatter | solution.py:35
  423.0 23.5 %all_gather.52 = bf16[1,256,1536]{2,1,0:T(8,128)(2,1)S(1)} all-gather(bf16[1,64,1536]{2,1,0:T(8,128)(2,1)} %reduce-scatter.30.cloned.1.call-done), channel_id=1, replica_groups=mesh['section'=2,'row'=4,'col'=4] {'row'}, dimensions={1}, use_global_device_ids=true | all-gather | bytes 983040 | tf_op jit(solution)/shard_map/all_gather | solution.py:50
  453.5 24.9 %all_gather.51 = bf16[1,256,1536]{2,1,0:T(8,128)(2,1)S(1)} all-gather(bf16[1,64,1536]{2,1,0:T(8,128)(2,1)} %reduce-scatter.26.cloned.1.call-done), channel_id=1, replica_groups=mesh['section'=2,'row'=4,'col'=4] {'row'}, dimensions={1}, use_global_device_ids=true | all-gather | bytes 983040 | tf_op jit(solution)/shard_map/all_gather | solution.py:51
  487.6 25.0 %all_gather.53 = bf16[1,256,1536]{2,1,0:T(8,128)(2,1)S(1)} all-gather(bf16[1,64,1536]{2,1,0:T(8,128)(2,1)S(1)} %bitcast.280), channel_id=1, replica_groups=mesh['section'=2,'row'=4,'col'=4] {'row'}, dimensions={1}, use_global_device_ids=true | all-gather | bytes 983040 | tf_op jit(solution)/shard_map/all_gather | solution.py:68
  512.6 42.9 %all-gather.6.cloned.1.call-done = bf16[1,256,6144]{2,1,0:T(8,128)(2,1)} async-done(((bf16[1,64,6144]{2,1,0:T(8,128)(2,1)}), bf16[1,256,6144]{2,1,0:T(8,128)(2,1)}) %all-gather.6.cloned.1.call-update) | async-done | bytes 3145744 | tf_op jit(solution)/shard_map/all_gather | solution.py:69
  570.1 22.5 %reduce-scatter.34.cloned.1.call-done = bf16[1,64,1536]{2,1,0:T(8,128)(2,1)} async-done(((bf16[1,256,1536]{2,1,0:T(8,128)(2,1)}), bf16[1,64,1536]{2,1,0:T(8,128)(2,1)}) %reduce-scatter.34.cloned.1.call-update) | async-done | bytes 196624 | tf_op jit(solution)/shard_map/reduce_scatter | solution.py:74
  648.2 45.0 %reduce-scatter.42.cloned.1.call-done = bf16[1,64,6144]{2,1,0:T(8,128)(2,1)} async-done(((bf16[1,256,6144]{2,1,0:T(8,128)(2,1)}), bf16[1,64,6144]{2,1,0:T(8,128)(2,1)}) %reduce-scatter.42.cloned.1.call-update) | async-done | bytes 786448 | tf_op jit(solution)/shard_map/reduce_scatter | solution.py:41
  698.4 20.1 %reduce-scatter.40.cloned.1.call-done = bf16[1,64,1536]{2,1,0:T(8,128)(2,1)} async-done(((bf16[1,256,1536]{2,1,0:T(8,128)(2,1)}), bf16[1,64,1536]{2,1,0:T(8,128)(2,1)}) %reduce-scatter.40.cloned.1.call-update) | async-done | bytes 196624 | tf_op jit(solution)/shard_map/reduce_scatter | solution.py:35
  718.4 23.7 %all_gather.57 = bf16[1,256,1536]{2,1,0:T(8,128)(2,1)S(1)} all-gather(bf16[1,64,1536]{2,1,0:T(8,128)(2,1)} %reduce-scatter.40.cloned.1.call-done), channel_id=1, replica_groups=mesh['section'=2,'row'=4,'col'=4] {'row'}, dimensions={1}, use_global_device_ids=true | all-gather | bytes 983040 | tf_op jit(solution)/shard_map/all_gather | solution.py:50
  748.9 23.8 %all_gather.56 = bf16[1,256,1536]{2,1,0:T(8,128)(2,1)S(1)} all-gather(bf16[1,64,1536]{2,1,0:T(8,128)(2,1)} %reduce-scatter.36.cloned.1.call-done), channel_id=1, replica_groups=mesh['section'=2,'row'=4,'col'=4] {'row'}, dimensions={1}, use_global_device_ids=true | all-gather | bytes 983040 | tf_op jit(solution)/shard_map/all_gather | solution.py:51
  782.6 25.7 %all_gather.58 = bf16[1,256,1536]{2,1,0:T(8,128)(2,1)S(1)} all-gather(bf16[1,64,1536]{2,1,0:T(8,128)(2,1)S(1)} %bitcast.281), channel_id=1, replica_groups=mesh['section'=2,'row'=4,'col'=4] {'row'}, dimensions={1}, use_global_device_ids=true | all-gather | bytes 983040 | tf_op jit(solution)/shard_map/all_gather | solution.py:68
  808.2 42.3 %all-gather.8.cloned.1.call-done = bf16[1,256,6144]{2,1,0:T(8,128)(2,1)} async-done(((bf16[1,64,6144]{2,1,0:T(8,128)(2,1)}), bf16[1,256,6144]{2,1,0:T(8,128)(2,1)}) %all-gather.8.cloned.1.call-update) | async-done | bytes 3145744 | tf_op jit(solution)/shard_map/all_gather | solution.py:69
  865.0 22.6 %reduce-scatter.44.cloned.1.call-done = bf16[1,64,1536]{2,1,0:T(8,128)(2,1)} async-done(((bf16[1,256,1536]{2,1,0:T(8,128)(2,1)}), bf16[1,64,1536]{2,1,0:T(8,128)(2,1)}) %reduce-scatter.44.cloned.1.call-update) | async-done | bytes 196624 | tf_op jit(solution)/shard_map/reduce_scatter | solution.py:74
  (112 shorter events, 233.7 us)
Async XLA Ops:
  6.5 95.6 %reduce-scatter.22.cloned.1.call-start = ((), (), s32[]{:S(2)}) async-start(), calls=%async_computation.18 | async-start | bytes 3932160 | tf_op jit(solution)/shard_map/reduce_scatter | solution.py:41
  44.3 83.2 %reduce-scatter.20.cloned.1.call-start = ((), (), s32[]{:S(2)}) async-start(), calls=%async_computation.17 | async-start | bytes 983040 | tf_op jit(solution)/shard_map/reduce_scatter | solution.py:35
  49.0 109.1 %reduce-scatter.16.cloned.1.call-start = ((), (), s32[]{:S(2)}) async-start(), calls=%async_computation.15 | async-start | bytes 983040 | tf_op jit(solution)/shard_map/reduce_scatter | solution.py:38
  53.6 135.2 %reduce-scatter.18.cloned.1.call-start = ((), (), s32[]{:S(2)}) async-start(), calls=%async_computation.16 | async-start | bytes 983040 | tf_op jit(solution)/shard_map/reduce_scatter | solution.py:32
  58.4 201.6 %all-gather.4.cloned.1.call-start = ((), (), s32[]{:S(2)}) async-start(), calls=%async_computation.19 | async-start | bytes 3932160 | tf_op jit(solution)/shard_map/all_gather | solution.py:69
  107.3 189.8 %reduce-scatter.24.cloned.1.call-start = ((), (), s32[]{:S(2)}) async-start(), calls=%async_computation.20 | async-start | bytes 983040 | tf_op jit(solution)/shard_map/reduce_scatter | solution.py:74
  269.9 27.2 %copy-start = (bf16[2,64,1536]{2,1,0:T(8,128)(2,1)S(1)}, bf16[2,64,1536]{2,1,0:T(8,128)(2,1)}, u32[]{:S(2)}) copy-start(bf16[2,64,1536]{2,1,0:T(8,128)(2,1)} %param.8) | copy-start | bytes 1179652
  274.6 123.1 %reduce-scatter.32.cloned.1.call-start = ((), (), s32[]{:S(2)}) async-start(), calls=%async_computation.24 | async-start | bytes 3932160 | tf_op jit(solution)/shard_map/reduce_scatter | solution.py:41
  298.1 7.3 collective-permute-start
  337.9 85.1 %reduce-scatter.30.cloned.1.call-start = ((), (), s32[]{:S(2)}) async-start(), calls=%async_computation.23 | async-start | bytes 983040 | tf_op jit(solution)/shard_map/reduce_scatter | solution.py:35
  342.6 110.9 %reduce-scatter.26.cloned.1.call-start = ((), (), s32[]{:S(2)}) async-start(), calls=%async_computation.21 | async-start | bytes 983040 | tf_op jit(solution)/shard_map/reduce_scatter | solution.py:38
  347.7 136.8 %reduce-scatter.28.cloned.1.call-start = ((), (), s32[]{:S(2)}) async-start(), calls=%async_computation.22 | async-start | bytes 983040 | tf_op jit(solution)/shard_map/reduce_scatter | solution.py:32
  352.4 203.2 %all-gather.6.cloned.1.call-start = ((), (), s32[]{:S(2)}) async-start(), calls=%async_computation.25 | async-start | bytes 3932160 | tf_op jit(solution)/shard_map/all_gather | solution.py:69
  402.8 189.8 %reduce-scatter.34.cloned.1.call-start = ((), (), s32[]{:S(2)}) async-start(), calls=%async_computation.26 | async-start | bytes 983040 | tf_op jit(solution)/shard_map/reduce_scatter | solution.py:74
  570.1 123.1 %reduce-scatter.42.cloned.1.call-start = ((), (), s32[]{:S(2)}) async-start(), calls=%async_computation.30 | async-start | bytes 3932160 | tf_op jit(solution)/shard_map/reduce_scatter | solution.py:41
  593.6 7.4 collective-permute-start.1
  633.4 85.0 %reduce-scatter.40.cloned.1.call-start = ((), (), s32[]{:S(2)}) async-start(), calls=%async_computation.29 | async-start | bytes 983040 | tf_op jit(solution)/shard_map/reduce_scatter | solution.py:35
  638.1 110.8 %reduce-scatter.36.cloned.1.call-start = ((), (), s32[]{:S(2)}) async-start(), calls=%async_computation.27 | async-start | bytes 983040 | tf_op jit(solution)/shard_map/reduce_scatter | solution.py:38
  643.2 136.3 %reduce-scatter.38.cloned.1.call-start = ((), (), s32[]{:S(2)}) async-start(), calls=%async_computation.28 | async-start | bytes 983040 | tf_op jit(solution)/shard_map/reduce_scatter | solution.py:32
  647.9 202.6 %all-gather.8.cloned.1.call-start = ((), (), s32[]{:S(2)}) async-start(), calls=%async_computation.31 | async-start | bytes 3932160 | tf_op jit(solution)/shard_map/all_gather | solution.py:69
  698.3 189.3 %reduce-scatter.44.cloned.1.call-start = ((), (), s32[]{:S(2)}) async-start(), calls=%async_computation.32 | async-start | bytes 983040 | tf_op jit(solution)/shard_map/reduce_scatter | solution.py:74
Sparse Core Ops, SparseCore 0:
  44.4 57.6 reduce-scatter.21
  104.4 23.0 reduce-scatter.19
  129.8 28.1 reduce-scatter.15
  160.2 28.6 reduce-scatter.17
  190.3 69.6 all-gather.3
  274.7 22.3 reduce-scatter.23
  338.1 59.5 reduce-scatter.31
  400.0 23.0 reduce-scatter.29
  425.3 28.1 reduce-scatter.25
  455.7 28.7 reduce-scatter.27
  486.1 69.4 all-gather.5
  570.2 22.3 reduce-scatter.33
  633.5 59.5 reduce-scatter.41
  695.3 23.0 reduce-scatter.39
  720.6 28.2 reduce-scatter.35
  751.1 28.3 reduce-scatter.37
  780.9 69.5 all-gather.7
  865.1 22.4 reduce-scatter.43
where the time goes:
time: 905 us; the launch traced here: 897 us
  waiting for transfers between devices  436 us (48%)
  blocking collectives  281 us (31%)
  matrix products  129 us (14%)
  other arithmetic  23.7 us (3%)
  between operations  14.3 us (2%)
    reduce_scatter x3, waiting for transfers between devices, layer(): lax.psum_scatter(part_m.astype(jnp.bfloat16), 'row', scatter_dimension=1,...  134 us
    all_gather x3, waiting for transfers between devices, layer(): lax.all_gather(act, 'row', axis=1, tiled=True)  128 us
    all_gather x3, blocking collectives, layer(): lax.all_gather(attn, 'row', axis=1, tiled=True)  75.9 us
    all_gather x3, blocking collectives, layer(): lax.all_gather(valued, 'row', axis=1, tiled=True)  73.1 us
    all_gather x3, blocking collectives, layer(): lax.all_gather(keyed, 'row', axis=1, tiled=True)  70.7 us
    reduce_scatter x3, waiting for transfers between devices, layer(): lax.psum_scatter(mixed.astype(jnp.bfloat16), 'col', scatter_dimension=1,...  67.6 us
    reduce_scatter x3, waiting for transfers between devices, layer(): lax.psum_scatter(part_k.astype(jnp.bfloat16), 'row', scatter_dimension=1,...  60.4 us
    dot_general x3, matrix products, layer(): part_m = jnp.dot(gathered, wup, preferred_element_type=jnp.float32)  38.3 us
  transfers between devices with their start and end apart: 20, of which 20 were waited for; matrix products, arithmetic and copies ran while one was open for 8% of the time, Pallas kernels for 0%

commit v1 on v0

--- a/solution.py
+++ b/solution.py
@@ -1,6 +1,10 @@
+import functools
+
 import jax
 import jax.numpy as jnp
 from jax import lax
+from jax.experimental import pallas as pl
+from jax.experimental.pallas import tpu as pltpu
 from jax.sharding import PartitionSpec as P
 
 D = 6144
@@ -8,6 +12,425 @@
 
 
 EPS = 1e-06
+MESH = pl.DeviceIdType.MESH
+PIECE = 16
+SKEW = 3
+VMEM_BYTES = 56 * 1024 * 1024
+
+
+def params(collective_id):
+    return pltpu.CompilerParams(
+        collective_id=collective_id, has_side_effects=True, vmem_limit_bytes=VMEM_BYTES
+    )
+
+
+def vmem():
+    return pl.BlockSpec(memory_space=pltpu.VMEM)
+
+
+def greet_peers(axes):
+    barrier = pltpu.get_barrier_semaphore()
+    total = 0
+    for axis, count in axes:
+        me = lax.axis_index(axis)
+        for step in range(1, count):
+            pl.semaphore_signal(
+                barrier, inc=1, device_id={axis: lax.rem(me + step, count)}, device_id_type=MESH
+            )
+            total += 1
+    pl.semaphore_wait(barrier, total)
+
+
+def greet_line(me, count):
+    barrier = pltpu.get_barrier_semaphore()
+
+    @pl.when(me > 0)
+    def _():
+        pl.semaphore_signal(barrier, inc=1, device_id={"row": me - 1}, device_id_type=MESH)
+
+    @pl.when(me < count - 1)
+    def _():
+        pl.semaphore_signal(barrier, inc=1, device_id={"row": me + 1}, device_id_type=MESH)
+
+    pl.semaphore_wait(barrier, jnp.where(jnp.logical_and(me > 0, me < count - 1), 2, 1))
+
+
+def norm_kernel(rows, cols, x_ref, gain_ref, out_ref, mine, stats, stat_send, stat_recv, send, recv, local_sem):
+    me_row, me_col = lax.axis_index("row"), lax.axis_index("col")
+    patches, width = x_ref.shape
+    greet_peers((("row", rows), ("col", cols)))
+    xf = x_ref[...].astype(jnp.float32)
+    total = jnp.sum(xf, axis=-1, keepdims=True)
+    square = jnp.sum(xf * xf, axis=-1, keepdims=True)
+    lane = lax.broadcasted_iota(jnp.int32, (patches, 128), 1)
+    stats[0] = jnp.where(lane < 64, total, square)
+    copies = []
+    for step in range(1, rows):
+        copy = pltpu.make_async_remote_copy(
+            src_ref=stats.at[0],
+            dst_ref=stats.at[step],
+            send_sem=stat_send.at[step],
+            recv_sem=stat_recv.at[step],
+            device_id={"row": lax.rem(me_row + step, rows)},
+            device_id_type=MESH,
+        )
+        copy.start()
+        copies.append(copy)
+    for copy in copies:
+        copy.wait()
+    both = stats[0]
+    for step in range(1, rows):
+        both = both + stats[step]
+    mean = both[:, 0:1] / D
+    var = jnp.maximum(both[:, 64:65] / D - mean * mean, 0.0)
+    mine[...] = ((xf - mean) * lax.rsqrt(var + EPS) * gain_ref[...]).astype(jnp.bfloat16)
+    place = pl.ds(pl.multiple_of(me_col * patches, patches), patches)
+    keep = pltpu.make_async_copy(mine, out_ref.at[place], local_sem)
+    keep.start()
+    copies = []
+    for step in range(1, cols):
+        copy = pltpu.make_async_remote_copy(
+            src_ref=mine,
+            dst_ref=out_ref.at[place],
+            send_sem=send.at[step],
+            recv_sem=recv.at[step],
+            device_id={"col": lax.rem(me_col + step, cols)},
+            device_id_type=MESH,
+        )
+        copy.start()
+        copies.append(copy)
+    for copy in copies:
+        copy.wait()
+    keep.wait()
+
+
+def norm_gather(x, gain, rows, cols):
+    patches, width = x.shape
+    return pl.pallas_call(
+        functools.partial(norm_kernel, rows, cols),
+        out_shape=jax.ShapeDtypeStruct((patches * cols, width), jnp.bfloat16),
+        in_specs=[vmem(), vmem()],
+        out_specs=vmem(),
+        scratch_shapes=[
+            pltpu.VMEM((patches, width), jnp.bfloat16),
+            pltpu.VMEM((rows, patches, 128), jnp.float32),
+            pltpu.SemaphoreType.DMA((rows,)),
+            pltpu.SemaphoreType.DMA((rows,)),
+            pltpu.SemaphoreType.DMA((cols,)),
+            pltpu.SemaphoreType.DMA((cols,)),
+            pltpu.SemaphoreType.DMA,
+        ],
+        compiler_params=params(0),
+    )(x, gain)
+
+
+def reduce_kernel(rows, q_ref, k_ref, v_ref, m_ref, out_ref, low, high, low_send, low_recv, high_send, high_recv):
+    me = lax.axis_index("row")
+    last = rows - 1
+    pieces = q_ref.shape[0] // PIECE
+    greet_line(me, rows)
+
+    def copy_of(held, send, recv, p, target):
+        place = pl.ds(pl.multiple_of(p * PIECE, PIECE), PIECE)
+        return pltpu.make_async_remote_copy(
+            src_ref=held.at[place],
+            dst_ref=held.at[place],
+            send_sem=send.at[p],
+            recv_sem=recv.at[p],
+            device_id={"row": target},
+            device_id_type=MESH,
+        )
+
+    def low_copy(p):
+        return copy_of(low, low_send, low_recv, p, jnp.maximum(me - 1, 0))
+
+    def high_copy(p):
+        return copy_of(high, high_send, high_recv, p, jnp.minimum(me + 1, last))
+
+    def add(held, p, side, is_source, is_sink):
+        place = pl.ds(pl.multiple_of(p * PIECE, PIECE), PIECE)
+        offset = 0
+        for ref in (q_ref, k_ref, v_ref, m_ref):
+            half = ref.shape[1] // 2
+            mine = ref[place, side * half : (side + 1) * half]
+            columns = slice(offset, offset + half)
+            offset += half
+
+            @pl.when(is_source)
+            def _():
+                held[place, columns] = mine
+
+            @pl.when(jnp.logical_not(is_source))
+            def _():
+                total = mine.astype(jnp.float32) + held[place, columns].astype(jnp.float32)
+
+                @pl.when(is_sink)
+                def _():
+                    out_ref[place, columns] = total.astype(jnp.bfloat16)
+
+                @pl.when(jnp.logical_not(is_sink))
+                def _():
+                    held[place, columns] = total.astype(jnp.bfloat16)
+
+    def step(s, carry):
+        p_low = s - SKEW * (last - me)
+        p_high = s - SKEW * me
+        low_on = jnp.logical_and(p_low >= 0, p_low < pieces)
+        high_on = jnp.logical_and(p_high >= 0, p_high < pieces)
+
+        @pl.when(low_on)
+        def _():
+            @pl.when(me < last)
+            def _():
+                low_copy(p_low).wait_recv()
+
+            add(low, p_low, 0, me == last, me == 0)
+
+        @pl.when(high_on)
+        def _():
+            @pl.when(me > 0)
+            def _():
+                high_copy(p_high).wait_recv()
+
+            add(high, p_high, 1, me == 0, me == last)
+
+        @pl.when(jnp.logical_and(low_on, me > 0))
+        def _():
+            low_copy(p_low).start()
+
+        @pl.when(jnp.logical_and(high_on, me < last))
+        def _():
+            high_copy(p_high).start()
+
+        return carry
+
+    lax.fori_loop(0, pieces + SKEW * last, step, 0)
+
+    def drain(p, carry):
+        @pl.when(me > 0)
+        def _():
+            low_copy(p).wait_send()
+
+        @pl.when(me < last)
+        def _():
+            high_copy(p).wait_send()
+
+        return carry
+
+    lax.fori_loop(0, pieces, drain, 0)
+
+
+def reduce_line(parts, rows):
+    patches = parts[0].shape[0]
+    width = sum(part.shape[1] for part in parts) // 2
+    pieces = patches // PIECE
+    return pl.pallas_call(
+        functools.partial(reduce_kernel, rows),
+        out_shape=jax.ShapeDtypeStruct((patches, width), jnp.bfloat16),
+        in_specs=[vmem()] * len(parts),
+        out_specs=vmem(),
+        scratch_shapes=[
+            pltpu.VMEM((patches, width), jnp.bfloat16),
+            pltpu.VMEM((patches, width), jnp.bfloat16),
+        ]
+        + [pltpu.SemaphoreType.DMA((pieces,))] * 4,
+        compiler_params=params(1),
+    )(*parts)
+
+
+def spread_kernel(rows, attn_ref, act_ref, attn_out, act_out, sems, local_sem):
+    me = lax.axis_index("row")
+    last = rows - 1
+    pieces = attn_ref.shape[0] // PIECE
+    greet_line(me, rows)
+    pairs = ((attn_ref, attn_out), (act_ref, act_out))
+
+    def piece_of(ref, p, side):
+        half = ref.shape[1] // 2
+        return ref.at[pl.ds(pl.multiple_of(p * PIECE, PIECE), PIECE), pl.ds(side * half, half)]
+
+    def copies(p, side, own, target):
+        out = []
+        for index, (source, full) in enumerate(pairs):
+            place = piece_of(full, p, side)
+            src = source.at[pl.ds(pl.multiple_of(p * PIECE, PIECE), PIECE)] if own else place
+            out.append(
+                pltpu.make_async_remote_copy(
+                    src_ref=src,
+                    dst_ref=place,
+                    send_sem=sems.at[0, side, index, p],
+                    recv_sem=sems.at[1, side, index, p],
+                    device_id={"row": target},
+                    device_id_type=MESH,
+                )
+            )
+        return out
+
+    up, down = jnp.minimum(me + 1, last), jnp.maximum(me - 1, 0)
+
+    for side, owner, target in ((0, 0, up), (1, last, down)):
+
+        @pl.when(me == owner)
+        def _():
+            for index, (source, full) in enumerate(pairs):
+                half = full.shape[1] // 2
+                pltpu.make_async_copy(
+                    source, full.at[:, pl.ds(side * half, half)], local_sem.at[index]
+                ).start()
+
+            def push(p, carry):
+                for copy in copies(p, side, True, target):
+                    copy.start()
+                return carry
+
+            lax.fori_loop(0, pieces, push, 0)
+
+    def step(s, carry):
+        for side, hops, target, end in ((0, me, up, last), (1, last - me, down, 0)):
+            p = s - SKEW * hops
+
+            @pl.when(jnp.logical_and(hops > 0, jnp.logical_and(p >= 0, p < pieces)))
+            def _():
+                moved = copies(p, side, False, target)
+                for copy in moved:
+                    copy.wait_recv()
+
+                @pl.when(me != end)
+                def _():
+                    for copy in moved:
+                        copy.start()
+
+        return carry
+
+    lax.fori_loop(0, pieces + SKEW * last, step, 0)
+
+    def drain(p, carry):
+        for side, target, end in ((0, up, last), (1, down, 0)):
+
+            @pl.when(me != end)
+            def _():
+                for copy in copies(p, side, False, target):
+                    copy.wait_send()
+
+        return carry
+
+    lax.fori_loop(0, pieces, drain, 0)
+    for side, owner in ((0, 0), (1, last)):
+
+        @pl.when(me == owner)
+        def _():
+            for index, (source, full) in enumerate(pairs):
+                half = full.shape[1] // 2
+                pltpu.make_async_copy(
+                    source, full.at[:, pl.ds(side * half, half)], local_sem.at[index]
+                ).wait()
+
+
+def spread_line(attn, act, rows):
+    patches = attn.shape[0]
+    pieces = patches // PIECE
+    return pl.pallas_call(
+        functools.partial(spread_kernel, rows),
+        out_shape=[
+            jax.ShapeDtypeStruct((patches, 2 * value.shape[1]), value.dtype) for value in (attn, act)
+        ],
+        in_specs=[vmem(), vmem()],
+        out_specs=[vmem(), vmem()],
+        scratch_shapes=[
+            pltpu.SemaphoreType.DMA((2, 2, 2, pieces)),
+            pltpu.SemaphoreType.DMA((2,)),
+        ],
+        compiler_params=params(2),
+    )(attn, act)
+
+
+def finish_kernel(cols, part_ref, x_ref, out_ref, held, send, recv):
+    me = lax.axis_index("col")
+    patches = x_ref.shape[0]
+    greet_peers((("col", cols),))
+
+    def block(owner):
+        return pl.ds(pl.multiple_of(owner * patches, patches), patches)
+
+    copies = []
+    for step in range(1, cols):
+        peer = lax.rem(me + step, cols)
+        copy = pltpu.make_async_remote_copy(
+            src_ref=part_ref.at[block(peer)],
+            dst_ref=held.at[step - 1],
+            send_sem=send.at[step],
+            recv_sem=recv.at[step],
+            device_id={"col": peer},
+            device_id_type=MESH,
+        )
+        copy.start()
+        copies.append(copy)
+    total = part_ref[block(me)].astype(jnp.float32)
+    for copy in copies:
+        copy.wait()
+    for step in range(1, cols):
+        total = total + held[step - 1].astype(jnp.float32)
+    out_ref[...] = (x_ref[...].astype(jnp.float32) + total).astype(jnp.bfloat16)
+
+
+def finish(part, x, cols):
+    patches, width = x.shape
+    return pl.pallas_call(
+        functools.partial(finish_kernel, cols),
+        out_shape=jax.ShapeDtypeStruct((patches, width), jnp.bfloat16),
+        in_specs=[vmem(), vmem()],
+        out_specs=vmem(),
+        scratch_shapes=[
+            pltpu.VMEM((cols - 1, patches, width), jnp.bfloat16),
+            pltpu.SemaphoreType.DMA((cols,)),
+            pltpu.SemaphoreType.DMA((cols,)),
+        ],
+        compiler_params=params(3),
+    )(part, x)
+
+
+def line_layer(x, weights):
+    gain, wq, wk, wv, wup, wout, wdown = weights
+    rows, cols = lax.axis_size("row"), lax.axis_size("col")
+    here = x[0]
+    gathered = norm_gather(here, gain[None], rows, cols)
+    parts = [
+        jnp.dot(gathered, w, preferred_element_type=jnp.float32).astype(jnp.bfloat16)
+        for w in (wq, wk, wv, wup)
+    ]
+    summed = reduce_line(parts, rows)
+    head_dim = D // HEADS
+    width = wq.shape[1] // 2
+    heads = width // head_dim
+    query, keyed, valued = (
+        summed[:, i * width : (i + 1) * width].reshape(-1, heads, head_dim) for i in range(3)
+    )
+    pre = summed[:, 3 * width :].astype(jnp.float32)
+    act = jax.nn.gelu(pre, approximate=False).astype(jnp.bfloat16)
+    scores = jnp.einsum("qhd,khd->hqk", query, keyed, preferred_element_type=jnp.float32) / jnp.sqrt(
+        jnp.float32(head_dim)
+    )
+    scores = scores - jnp.max(scores, axis=-1, keepdims=True)
+    expo = jnp.exp(scores)
+    probs = (expo / jnp.sum(expo, axis=-1, keepdims=True)).astype(jnp.bfloat16)
+    attn = jnp.einsum("hqk,khd->qhd", probs, valued, preferred_element_type=jnp.float32)
+    attn = attn.reshape(-1, width).astype(jnp.bfloat16)
+    attn_full, act_full = spread_line(attn, act, rows)
+    mixed = jnp.dot(attn_full, wout, preferred_element_type=jnp.float32) + jnp.dot(
+        act_full, wdown, preferred_element_type=jnp.float32
+    )
+    return finish(mixed.astype(jnp.bfloat16), here, cols)[None]
+
+
+def halves(x, wq, wup):
+    patches = x.shape[1]
+    return (
+        lax.axis_size("row") > 1
+        and lax.axis_size("col") > 1
+        and patches % PIECE == 0
+        and (wq.shape[1] // 2) % (D // HEADS) == 0
+        and (wup.shape[1] // 2) % 128 == 0
+    )
 
 
 def passed_along(value, axis, steps):
@@ -90,10 +513,11 @@
     ticks = images + sections - 1
     inbox = jnp.zeros_like(tokens[:1])
     positions = jnp.arange(images, dtype=jnp.int32)
+    step = line_layer if halves(tokens, w_query[0], w_up[0]) else layer
     for tick in range(ticks):
         fresh = tokens[min(tick, images - 1) : min(tick, images - 1) + 1]
         current = jnp.where(section == 0, fresh, inbox)
-        output = layer(current, weights)
+        output = step(current, weights)
         slot = tick - section
         result = jnp.where((positions == slot)[:, None, None], output, result)
         if tick + 1 < ticks:

time: 905 us -> 694 us (0.77)
  Pallas kernels: 0 us -> 524 us
  waiting for transfers between devices: 436 us -> 10.4 us
  blocking collectives: 281 us -> 0 us
  matrix products: 129 us -> 104 us
  between operations: 14.3 us -> 0.75 us
    pallas_call x0 -> x12, Pallas kernels: none -> 524 us  [the longest x3 252 us: reduce_line(): pl.pallas_call(functools.partial(reduce_kernel, rows), out_shape=jax.Shap...]
    reduce_scatter x15 -> x0, waiting for transfers between devices: 300 us -> none  [the longest x3 134 us: layer(): lax.psum_scatter(part_m.astype(jnp.bfloat16), 'row', scatter_dimension=1,...]
    all_gather x12 -> x0, blocking collectives: 244 us -> none  [the longest x3 75.9 us: layer(): lax.all_gather(attn, 'row', axis=1, tiled=True)]
    all_gather x3 -> x0, waiting for transfers between devices: 128 us -> none  [layer(): lax.all_gather(act, 'row', axis=1, tiled=True)]
    psum x3 -> x0, blocking collectives: 36.9 us -> none  [layer(): lax.psum((jnp.sum(xf, axis=-1), jnp.sum(xf * xf, axis=-1)), 'row')]
    dot_general x24 -> x21, matrix products: 129 us -> 102 us  [the longest x12 61.7 us: line_layer(): jnp.dot(gathered, w, preferred_element_type=jnp.float32)]
    convert_element_type x8 -> x3, other arithmetic: 18.7 us -> 25.7 us  [line_layer(): act = jax.nn.gelu(pre, approximate=False).astype(jnp.bfloat16)]
  transfers between devices with their start and end apart: 20 -> 2, of which waited for: 20 -> 2; matrix products, arithmetic and copies ran while one was open for 8% -> 0% of each run, Pallas kernels for 0% -> 0%
where the time goes in v1:
time: 694 us; the launch traced here: 686 us
  Pallas kernels  524 us (76%)
  matrix products  104 us (15%)
  other arithmetic  30.6 us (4%)
  waiting for transfers between devices  10.4 us (1%)
  local copies, waits for them, and re-layouts  8.38 us (1%)
  starting transfers between devices  8.34 us (1%)
    pallas_call x3, Pallas kernels, reduce_line(): pl.pallas_call(functools.partial(reduce_kernel, rows), out_shape=jax.Shap...  252 us
    pallas_call x3, Pallas kernels, spread_line(): pl.pallas_call(functools.partial(spread_kernel, rows), out_shape=[jax.Sha...  183 us
    dot_general x12, matrix products, line_layer(): jnp.dot(gathered, w, preferred_element_type=jnp.float32)  61.7 us
    pallas_call x3, Pallas kernels, norm_gather(): pl.pallas_call(functools.partial(norm_kernel, rows, cols), out_shape=jax....  52.2 us
    pallas_call x3, Pallas kernels, finish(): pl.pallas_call(functools.partial(finish_kernel, cols), out_shape=jax.Shap...  36 us
    dot_general x3, matrix products, line_layer(): jnp.dot(act_full, wdown, preferred_element_type=jnp.float32)  30 us
    convert_element_type x3, other arithmetic, line_layer(): act = jax.nn.gelu(pre, approximate=False).astype(jnp.bfloat16)  25.7 us
  transfers between devices with their start and end apart: 2, of which 2 were waited for; matrix products, arithmetic and copies ran while one was open for 0% of the time, Pallas kernels for 0%

profile of v1, /device:TPU:0, one launch (start us, length us, event | category | flops | bytes accessed | tf_op | source)
XLA Modules:
  0.0 686.4 jit_solution(48301203363860268)
XLA Ops:
  1.6 19.4 %shard_map.82 = bf16[256,1536]{1,0:T(8,128)(2,1)} custom-call(bf16[64,1536]{1,0:T(8,128)(2,1)} %select_bitcast_fusion.2.x_ref, f32[1,1536]{1,0:T(1,128)} %gain_ref.5), custom_call_target="tpu_custom_call" | custom-call | tf_op jit(solution)/shard_map/pallas_call | solution.py:109
  21.0 12.8 %fusion.15.m_ref = bf16[256,6144]{1,0:T(8,128)(2,1)} fusion(bf16[256,1536]{1,0:T(8,128)(2,1)} %shard_map.82, bf16[1,1536,6144]{2,1,0:T(8,128)(2,1)} %param.13), kind=kOutput, calls=%fused_computation.15 | convolution fusion | flops 4833411072 | bytes 22806528 | tf_op jit(solution)/shard_map/dot_general | solution.py:398
  40.8 84.4 %shard_map.83 = bf16[256,5376]{1,0:T(8,128)(2,1)} custom-call(bf16[256,1536]{1,0:T(8,128)(2,1)} %fusion.159.q_ref, bf16[256,1536]{1,0:T(8,128)(2,1)} %fusion.168.k_ref, bf16[256,1536]{1,0:T(8,128)(2,1)} %fusion.177.v_ref, bf16[256,6144]{1,0:T(8,128)(2,1)} %fusion.15.m_ref), custom_call_target="tpu_custom_call" | custom-call | tf_op jit(solution)/shard_map/pallas_call | solution.py:227
  126.6 8.6 %fusion.49.act_ref = bf16[256,3072]{1,0:T(8,128)(2,1)} fusion(bf16[256,5376]{1,0:T(8,128)(2,1)} %shard_map.83), kind=kLoop, calls=%fused_computation.52 | loop fusion | flops 51904512 | bytes 3145728 | tf_op jit(solution)/shard_map/convert_element_type | solution.py:409
  137.5 61.4 %shard_map.84 = (bf16[256,1536]{1,0:T(8,128)(2,1)}, bf16[256,6144]{1,0:T(8,128)(2,1)}) custom-call(bf16[256,768]{1,0:T(8,128)(2,1)} %copy.30.attn_ref, bf16[256,3072]{1,0:T(8,128)(2,1)} %fusion.49.act_ref), custom_call_target="tpu_custom_call" | custom-call | tf_op jit(solution)/shard_map/pallas_call | solution.py:332
  199.0 10.0 %fusion.7 = f32[256,1536]{1,0:T(8,128)S(1)} fusion(bf16[256,6144]{1,0:T(8,128)(2,1)} %get-tuple-element.12, bf16[1,6144,1536]{2,1,0:T(8,128)(2,1)} %param.15), kind=kOutput, calls=%fused_computation.7 | convolution fusion | flops 4831838208 | bytes 23592960 | tf_op jit(solution)/shard_map/dot_general | solution.py:419
  211.3 12.2 %shard_map.85 = bf16[64,1536]{1,0:T(8,128)(2,1)} custom-call(bf16[256,1536]{1,0:T(8,128)(2,1)} %fusion.156.part_ref, bf16[64,1536]{1,0:T(8,128)(2,1)} %select_bitcast_fusion.2.x_ref), custom_call_target="tpu_custom_call" | custom-call | tf_op jit(solution)/shard_map/pallas_call | solution.py:378
  227.0 5.5 collective-permute-done
  233.2 16.3 %shard_map.86 = bf16[256,1536]{1,0:T(8,128)(2,1)} custom-call(bf16[64,1536]{1,0:T(8,128)(2,1)} %select_bitcast_fusion.1.x_ref, f32[1,1536]{1,0:T(1,128)} %gain_ref.5), custom_call_target="tpu_custom_call" | custom-call | tf_op jit(solution)/shard_map/pallas_call | solution.py:109
  249.5 10.5 %fusion.18.m_ref = bf16[256,6144]{1,0:T(8,128)(2,1)} fusion(bf16[256,1536]{1,0:T(8,128)(2,1)} %shard_map.86, bf16[1,1536,6144]{2,1,0:T(8,128)(2,1)} %param.13), kind=kOutput, calls=%fused_computation.16 | convolution fusion | flops 4833411072 | bytes 22806528 | tf_op jit(solution)/shard_map/dot_general | solution.py:398
  271.8 83.3 %shard_map.87 = bf16[256,5376]{1,0:T(8,128)(2,1)} custom-call(bf16[256,1536]{1,0:T(8,128)(2,1)} %fusion.162.q_ref, bf16[256,1536]{1,0:T(8,128)(2,1)} %fusion.171.k_ref, bf16[256,1536]{1,0:T(8,128)(2,1)} %fusion.180.v_ref, bf16[256,6144]{1,0:T(8,128)(2,1)} %fusion.18.m_ref), custom_call_target="tpu_custom_call" | custom-call | tf_op jit(solution)/shard_map/pallas_call | solution.py:227
  356.4 8.6 %fusion.80.act_ref = bf16[256,3072]{1,0:T(8,128)(2,1)} fusion(bf16[256,5376]{1,0:T(8,128)(2,1)} %shard_map.87), kind=kLoop, calls=%fused_computation.83 | loop fusion | flops 51904512 | bytes 3145728 | tf_op jit(solution)/shard_map/convert_element_type | solution.py:409
  367.4 61.3 %shard_map.88 = (bf16[256,1536]{1,0:T(8,128)(2,1)}, bf16[256,6144]{1,0:T(8,128)(2,1)}) custom-call(bf16[256,768]{1,0:T(8,128)(2,1)} %copy.37.attn_ref, bf16[256,3072]{1,0:T(8,128)(2,1)} %fusion.80.act_ref), custom_call_target="tpu_custom_call" | custom-call | tf_op jit(solution)/shard_map/pallas_call | solution.py:332
  428.8 10.0 %fusion.5 = f32[256,1536]{1,0:T(8,128)S(1)} fusion(bf16[256,6144]{1,0:T(8,128)(2,1)} %get-tuple-element.14, bf16[1,6144,1536]{2,1,0:T(8,128)(2,1)} %param.15), kind=kOutput, calls=%fused_computation.5 | convolution fusion | flops 4831838208 | bytes 23592960 | tf_op jit(solution)/shard_map/dot_general | solution.py:419
  443.5 11.8 %shard_map.89 = bf16[64,1536]{1,0:T(8,128)(2,1)} custom-call(bf16[256,1536]{1,0:T(8,128)(2,1)} %fusion.153.part_ref, bf16[64,1536]{1,0:T(8,128)(2,1)} %select_bitcast_fusion.1.x_ref), custom_call_target="tpu_custom_call" | custom-call | tf_op jit(solution)/shard_map/pallas_call | solution.py:378
  455.3 4.9 collective-permute-start.1
  460.3 4.9 collective-permute-done.1
  465.9 16.6 %shard_map.90 = bf16[256,1536]{1,0:T(8,128)(2,1)} custom-call(bf16[64,1536]{1,0:T(8,128)(2,1)} %select_bitcast_fusion.x_ref, f32[1,1536]{1,0:T(1,128)} %gain_ref.5), custom_call_target="tpu_custom_call" | custom-call | tf_op jit(solution)/shard_map/pallas_call | solution.py:109
  482.6 12.8 %fusion.21.m_ref = bf16[256,6144]{1,0:T(8,128)(2,1)} fusion(bf16[256,1536]{1,0:T(8,128)(2,1)} %shard_map.90, bf16[1,1536,6144]{2,1,0:T(8,128)(2,1)} %param.13), kind=kOutput, calls=%fused_computation.17 | convolution fusion | flops 4833411072 | bytes 22806528 | tf_op jit(solution)/shard_map/dot_general | solution.py:398
  502.4 84.5 %shard_map.91 = bf16[256,5376]{1,0:T(8,128)(2,1)} custom-call(bf16[256,1536]{1,0:T(8,128)(2,1)} %fusion.165.q_ref, bf16[256,1536]{1,0:T(8,128)(2,1)} %fusion.174.k_ref, bf16[256,1536]{1,0:T(8,128)(2,1)} %fusion.183.v_ref, bf16[256,6144]{1,0:T(8,128)(2,1)} %fusion.21.m_ref), custom_call_target="tpu_custom_call" | custom-call | tf_op jit(solution)/shard_map/pallas_call | solution.py:227
  588.2 8.6 %fusion.111.act_ref = bf16[256,3072]{1,0:T(8,128)(2,1)} fusion(bf16[256,5376]{1,0:T(8,128)(2,1)} %shard_map.91), kind=kLoop, calls=%fused_computation.114 | loop fusion | flops 51904512 | bytes 3145728 | tf_op jit(solution)/shard_map/convert_element_type | solution.py:409
  599.2 60.7 %shard_map.92 = (bf16[256,1536]{1,0:T(8,128)(2,1)}, bf16[256,6144]{1,0:T(8,128)(2,1)}) custom-call(bf16[256,768]{1,0:T(8,128)(2,1)} %copy.44.attn_ref, bf16[256,3072]{1,0:T(8,128)(2,1)} %fusion.111.act_ref), custom_call_target="tpu_custom_call" | custom-call | tf_op jit(solution)/shard_map/pallas_call | solution.py:332
  659.9 10.0 %fusion.3 = f32[256,1536]{1,0:T(8,128)S(1)} fusion(bf16[256,6144]{1,0:T(8,128)(2,1)} %get-tuple-element.16, bf16[1,6144,1536]{2,1,0:T(8,128)(2,1)} %param.15), kind=kOutput, calls=%fused_computation.3 | convolution fusion | flops 4831838208 | bytes 23592960 | tf_op jit(solution)/shard_map/dot_general | solution.py:419
  672.3 12.0 %shard_map.93 = bf16[64,1536]{1,0:T(8,128)(2,1)} custom-call(bf16[256,1536]{1,0:T(8,128)(2,1)} %fusion.150.part_ref, bf16[64,1536]{1,0:T(8,128)(2,1)} %select_bitcast_fusion.x_ref), custom_call_target="tpu_custom_call" | custom-call | tf_op jit(solution)/shard_map/pallas_call | solution.py:378
  (103 shorter events, 54.6 us)
Async XLA Ops:
  1.6 32.2 %slice-start = ((s8[4718592]{0:T(1024)(128)(4,1)}), s8[524288]{0:T(1024)(128)(4,1)S(1)}, s32[]{:S(2)}) async-start(s8[4718592]{0:T(1024)(128)(4,1)} %bitcast.145), calls=%async_computation | async-start | bytes 1048576
  1.6 34.5 %slice-start.4 = ((s8[4718592]{0:T(1024)(128)(4,1)}), s8[4194304]{0:T(1024)(128)(4,1)S(1)}, s32[]{:S(2)}) async-start(s8[4718592]{0:T(1024)(128)(4,1)} %bitcast.149), calls=%async_computation.4 | async-start | bytes 8388608
  21.0 12.8 %copy-start.3 = (bf16[256,1536]{1,0:T(8,128)(2,1)S(1)}, bf16[256,1536]{1,0:T(8,128)(2,1)}, u32[]{:S(2)}) copy-start(bf16[256,1536]{1,0:T(8,128)(2,1)} %shard_map.82) | copy-start | bytes 2359300
  21.0 12.8 %slice-start.1 = ((s8[4718592]{0:T(1024)(128)(4,1)}), s8[4194304]{0:T(1024)(128)(4,1)S(1)}, s32[]{:S(2)}) async-start(s8[4718592]{0:T(1024)(128)(4,1)} %bitcast.145), calls=%async_computation.1 | async-start | bytes 8388608
  21.0 15.1 %slice-start.5 = ((s8[4718592]{0:T(1024)(128)(4,1)}), s8[524288]{0:T(1024)(128)(4,1)S(1)}, s32[]{:S(2)}) async-start(s8[4718592]{0:T(1024)(128)(4,1)} %bitcast.149), calls=%async_computation.5 | async-start | bytes 1048576
  137.5 71.5 %slice-start.14 = ((s8[4718592]{0:T(1024)(128)(4,1)}), s8[524288]{0:T(1024)(128)(4,1)S(1)}, s32[]{:S(2)}) async-start(s8[4718592]{0:T(1024)(128)(4,1)} %bitcast.159), calls=%async_computation.14 | async-start | bytes 1048576
  198.9 10.1 %slice-start.15 = ((s8[4718592]{0:T(1024)(128)(4,1)}), s8[4194304]{0:T(1024)(128)(4,1)S(1)}, s32[]{:S(2)}) async-start(s8[4718592]{0:T(1024)(128)(4,1)} %bitcast.159), calls=%async_computation.15 | async-start | bytes 8388608
  198.9 10.1 %copy-start.6 = (bf16[256,1536]{1,0:T(8,128)(2,1)S(1)}, bf16[256,1536]{1,0:T(8,128)(2,1)}, u32[]{:S(2)}) copy-start(bf16[256,1536]{1,0:T(8,128)(2,1)} %get-tuple-element.11) | copy-start | bytes 2359300
  209.0 23.5 %copy-start = (bf16[2,64,1536]{2,1,0:T(8,128)(2,1)S(1)}, bf16[2,64,1536]{2,1,0:T(8,128)(2,1)}, u32[]{:S(2)}) copy-start(bf16[2,64,1536]{2,1,0:T(8,128)(2,1)} %param.8) | copy-start | bytes 1179652
  223.6 9.0 %collective-permute-start = (bf16[1,64,1536]{2,1,0:T(8,128)(2,1)}, bf16[1,64,1536]{2,1,0:T(8,128)(2,1)S(1)}, u32[]{:S(2)}, u32[]{:S(2)}) collective-permute-start(bf16[1,64,1536]{2,1,0:T(8,128)(2,1)} %bitcast.131), channel_id=1, source_target_pairs={{0,16},{1,17},{2,18},{3,19},{4,20},{5,21},{6,22},{7,23},{8,24},{9,... | collective-permute-start | bytes 589832 | tf_op jit(solution)/shard_map/ppermute | solution.py:439
  249.5 10.5 %copy-start.4 = (bf16[256,1536]{1,0:T(8,128)(2,1)S(1)}, bf16[256,1536]{1,0:T(8,128)(2,1)}, u32[]{:S(2)}) copy-start(bf16[256,1536]{1,0:T(8,128)(2,1)} %shard_map.86) | copy-start | bytes 2359300
  260.0 9.5 %slice-start.10 = ((s8[4718592]{0:T(1024)(128)(4,1)}), s8[4194304]{0:T(1024)(128)(4,1)S(1)}, s32[]{:S(2)}) async-start(s8[4718592]{0:T(1024)(128)(4,1)} %bitcast.155), calls=%async_computation.10 | async-start | bytes 8388608
  428.8 10.0 %copy-start.7 = (bf16[256,1536]{1,0:T(8,128)(2,1)S(1)}, bf16[256,1536]{1,0:T(8,128)(2,1)}, u32[]{:S(2)}) copy-start(bf16[256,1536]{1,0:T(8,128)(2,1)} %get-tuple-element.13) | copy-start | bytes 2359300
  438.7 56.6 %slice-start.2 = ((s8[4718592]{0:T(1024)(128)(4,1)}), s8[524288]{0:T(1024)(128)(4,1)S(1)}, s32[]{:S(2)}) async-start(s8[4718592]{0:T(1024)(128)(4,1)} %bitcast.147), calls=%async_computation.2 | async-start | bytes 1048576
  438.7 59.0 %slice-start.6 = ((s8[4718592]{0:T(1024)(128)(4,1)}), s8[4194304]{0:T(1024)(128)(4,1)S(1)}, s32[]{:S(2)}) async-start(s8[4718592]{0:T(1024)(128)(4,1)} %bitcast.151), calls=%async_computation.6 | async-start | bytes 8388608
  455.3 9.9 %collective-permute-start.1 = (bf16[1,64,1536]{2,1,0:T(8,128)(2,1)}, bf16[1,64,1536]{2,1,0:T(8,128)(2,1)S(1)}, u32[]{:S(2)}, u32[]{:S(2)}) collective-permute-start(bf16[1,64,1536]{2,1,0:T(8,128)(2,1)} %bitcast.132), channel_id=1, source_target_pairs={{0,16},{1,17},{2,18},{3,19},{4,20},{5,21},{6,22},{7,23},{8,24},{9,... | collective-permute-start | bytes 589832 | tf_op jit(solution)/shard_map/ppermute | solution.py:439
  482.5 12.8 %copy-start.5 = (bf16[256,1536]{1,0:T(8,128)(2,1)S(1)}, bf16[256,1536]{1,0:T(8,128)(2,1)}, u32[]{:S(2)}) copy-start(bf16[256,1536]{1,0:T(8,128)(2,1)} %shard_map.90) | copy-start | bytes 2359300
  482.6 12.8 %slice-start.3 = ((s8[4718592]{0:T(1024)(128)(4,1)}), s8[4194304]{0:T(1024)(128)(4,1)S(1)}, s32[]{:S(2)}) async-start(s8[4718592]{0:T(1024)(128)(4,1)} %bitcast.147), calls=%async_computation.3 | async-start | bytes 8388608
  482.6 15.1 %slice-start.7 = ((s8[4718592]{0:T(1024)(128)(4,1)}), s8[524288]{0:T(1024)(128)(4,1)S(1)}, s32[]{:S(2)}) async-start(s8[4718592]{0:T(1024)(128)(4,1)} %bitcast.151), calls=%async_computation.7 | async-start | bytes 1048576
  598.0 72.0 %slice-start.16 = ((s8[4718592]{0:T(1024)(128)(4,1)}), s8[524288]{0:T(1024)(128)(4,1)S(1)}, s32[]{:S(2)}) async-start(s8[4718592]{0:T(1024)(128)(4,1)} %bitcast.161), calls=%async_computation.16 | async-start | bytes 1048576
  659.9 10.1 %slice-start.17 = ((s8[4718592]{0:T(1024)(128)(4,1)}), s8[4194304]{0:T(1024)(128)(4,1)S(1)}, s32[]{:S(2)}) async-start(s8[4718592]{0:T(1024)(128)(4,1)} %bitcast.161), calls=%async_computation.17 | async-start | bytes 8388608
  659.9 10.1 %copy-start.8 = (bf16[256,1536]{1,0:T(8,128)(2,1)S(1)}, bf16[256,1536]{1,0:T(8,128)(2,1)}, u32[]{:S(2)}) copy-start(bf16[256,1536]{1,0:T(8,128)(2,1)} %get-tuple-element.15) | copy-start | bytes 2359300
  670.0 14.3 %copy-start.1 = (bf16[64,1536]{1,0:T(8,128)(2,1)S(1)}, bf16[64,1536]{1,0:T(8,128)(2,1)}, u32[]{:S(2)}) copy-start(bf16[64,1536]{1,0:T(8,128)(2,1)} %shard_map.85) | copy-start | bytes 589828
  670.0 14.3 %copy-start.2 = (bf16[64,1536]{1,0:T(8,128)(2,1)S(1)}, bf16[64,1536]{1,0:T(8,128)(2,1)}, u32[]{:S(2)}) copy-start(bf16[64,1536]{1,0:T(8,128)(2,1)} %shard_map.89) | copy-start | bytes 589828
  (5 other events, 18.5 us)
